TPU v7x, 32 devices: a whole 2x2x4 slice. The times are simulated.
32 devices in a mesh: row: 8 (over y, x, core), col: 4 (over z).
Axes of the slice: x: 2, y: 2, z: 4, core: 2. Of those that a mesh axis runs over, the one named last changes fastest.
Arguments:
- surface: bfloat16 [16384, 16384], P('row', 'col'), may hold values from -0.0234375 to 0.0234375
- excitation: float32 [16384, 128], P(('row', 'col')), may hold values from -6 to 6
- dtn_blocks: bfloat16 [32, 1024, 1024], P(('row', 'col')), may hold values from -0.09375 to 0.09375
- interp_blocks: bfloat16 [32, 1024, 2048], P(('row', 'col')), may hold values from -0.09375 to 0.09375
- adjacency: int32 [32, 6], P(('row', 'col')), may hold values from 0 to 31, as said below
Outputs:
- solution: float32 [16384, 128], P(('row', 'col'))
- residual: float32 [16384, 128], P(('row', 'col'))
Inputs may be any that keep to these rules, and one draw needn't show every extreme that they name: `adjacency`: entry [s, k] names a subdomain of the same spatial group as s (equal index // 4); it may name s itself, which adds nothing.
All inputs are finite; a program needn't handle non-finite values.
Results may differ from a plain program's by a relative error of at most 0.02.
Values may be sent and summed in bfloat16 or wider, within the bound.
A program may use at most 64 MiB of HBM per device.

v0:
```python
import functools

import jax
import jax.numpy as jnp
from jax import lax
from jax.experimental import pallas as pl
from jax.experimental.pallas import tpu as pltpu
from jax.sharding import PartitionSpec as P

ITERS = 2
NADJ = 6

damping = 0.25
face_weight = 0.25
F32, BF16 = jnp.float32, jnp.bfloat16


def xor(a, b, bits):
    total = 0
    for i in range(bits):
        x, y = a // 2**i % 2, b // 2**i % 2
        total = total + (x + y - 2 * x * y) * 2**i
    return total


def gray(p, bits):
    return xor(p, p // 2, bits)


def ungray(g, bits):
    total, above = 0, 0
    for i in reversed(range(bits)):
        bit = g // 2**i % 2
        above = above + bit - 2 * above * bit
        total = total + above * 2**i
    return total


def kernel(
    R, n, tile,
    exc_hbm, interp_hbm, surf_hbm, dtn_hbm, adj,
    sol_ref, res_ref,
    exc, interp, surf, dtn, grp, colb, trc, acc, part, sbuf, rbuf,
    load_sem, g_ss, g_rs, t_ss, t_rs, c_ss, c_rs, p_ss, p_rs, r_ss, r_rs,
):
    half_n = n // 2
    bits = n.bit_length() - 1
    _, _, hs, ne = grp.shape[1:]
    m = interp.shape[0]
    rb = interp.shape[1]
    tiles = surf.shape[0] // tile
    r, c = lax.axis_index("row"), lax.axis_index("col")
    core, chip = r % 2, r // 2
    pos = ungray(xor(chip, c, bits), bits)
    right, left = (r, (c + 1) % n), (r, (c + n - 1) % n)
    partner = (chip * 2 + 1 - core, c)
    gnext = (xor(gray((pos + 1) % n, bits), c, bits) * 2 + core, c)
    gprev = (xor(gray((pos + n - 1) % n, bits), c, bits) * 2 + core, c)

    loads = [
        pltpu.make_async_copy(exc_hbm, exc, load_sem.at[0]),
        pltpu.make_async_copy(interp_hbm, interp, load_sem.at[1]),
    ]
    for i in range(tiles):
        rows = pl.ds(i * tile, tile)
        loads.append(pltpu.make_async_copy(surf_hbm.at[rows], surf.at[rows], load_sem.at[3 + i]))
    loads.append(pltpu.make_async_copy(dtn_hbm, dtn, load_sem.at[2]))
    for load in loads:
        load.start()

    barrier = pltpu.get_barrier_semaphore()
    for device in (left, right, partner, gnext, gprev):
        pl.semaphore_signal(barrier, inc=1, device_id=device, device_id_type=pl.DeviceIdType.MESH)
    pl.semaphore_wait(barrier, 5)

    def remote(src, dst, ss, rs, device):
        return pltpu.make_async_remote_copy(
            src_ref=src, dst_ref=dst, send_sem=ss, recv_sem=rs,
            device_id=device, device_id_type=pl.DeviceIdType.MESH,
        )

    def ring(buf, ss, rs, s, d, t, h, receive=False):
        hop = t if receive else t - 1
        owner = (c + n - hop) % n if d == 0 else (c + hop) % n
        block = buf.at[s, owner, h]
        return remote(block, block, ss.at[s, d, t - 1, h], rs.at[s, d, t - 1, h], right if d == 0 else left)

    def halves(d, t):
        if t == half_n:
            return (d,)
        return (d, 1 - d)

    waits = []

    def chain_copies(src, s, owner, delta, h):
        block = src.at[owner, h]
        dst = colb.at[s, core, owner, h]
        k = (s, delta, h)
        return (
            remote(block, dst, c_ss.at[k], c_rs.at[k], gnext if h == 0 else gprev),
            remote(block, dst, p_ss.at[k], p_rs.at[k], partner),
        )

    def chain_source(s, deltas):
        @pl.when(pos == 0)
        def _():
            for delta in deltas:
                for h in range(2):
                    on, _ = chain_copies(grp.at[s], s, (c + delta) % n, delta, h)
                    on.start()
            for delta in deltas:
                for h in range(2):
                    _, share = chain_copies(grp.at[s], s, (c + delta) % n, delta, h)
                    share.start()

    arrival = [0] + sorted(range(1, n), key=lambda k: min(k, n - k))

    def chain_relay(s, phase):
        for q in range(1, n):
            pieces = []
            for k, delta in enumerate(arrival):
                for h in range(2):
                    hops = q if h == 0 else n - q
                    own_phase = 2 if hops > 1 else (0 if k == 0 else 1)
                    if own_phase == phase:
                        pieces.append((k + hops, -hops, k, delta, h))
            pieces.sort()

            @pl.when(pos == q)
            def _():
                for _, _, _, delta, h in pieces:
                    on, share = chain_copies(colb.at[s, core], s, (c + delta) % n, delta, h)
                    on.wait_recv()
                    if q != (n - 1 if h == 0 else 1):
                        on.start()
                    share.start()

    def chain_sent(s):
        for delta in range(n):
            for h in range(2):
                on, share = chain_copies(colb.at[s, core], s, (c + delta) % n, delta, h)
                waits.append((pos != (n - 1 if h == 0 else 1), on))
                waits.append((None, share))

    def chain_done(s, owner, delta):
        for h in range(2):
            block = colb.at[s, 1 - core, owner, h]
            k = (s, delta, h)
            remote(block, block, p_ss.at[k], p_rs.at[k], partner).wait_recv()

    counts = []
    for p in range(n):
        count = jnp.float32(0)
        for k in range(NADJ):
            count = count + jnp.where(adj[0, k] % n == p, 1.0, 0.0).astype(F32)
        counts.append(count)

    def send_own(s, h, value):
        grp[s, c, h] = value.astype(BF16)
        for d in range(2):
            copy = ring(grp, g_ss, g_rs, s, d, 1, h)
            copy.start()
            waits.append((None, copy))

    loads[0].wait()
    for s in range(ITERS):
        base = exc if s == 0 else sol_ref
        if s == 0:
            for h in range(2):
                send_own(0, h, exc[pl.ds(h * hs, hs), :])
        chain_source(s, arrival[:1])

        for t in range(2, half_n + 1):
            for i in range(2):
                for d in range(2):
                    h = halves(d, t)
                    if i < len(h):
                        copy = ring(grp, g_ss, g_rs, s, d, t, h[i])
                        ring(grp, g_ss, g_rs, s, d, t - 1, h[i], True).wait_recv()
                        copy.start()
                        waits.append((None, copy))
            if t > 1:
                for d in range(2):
                    for h in halves(d, t - 1):
                        if h not in halves(d, t):
                            ring(grp, g_ss, g_rs, s, d, t - 1, h, True).wait_recv()
        for d in range(2):
            for h in halves(d, half_n):
                ring(grp, g_ss, g_rs, s, d, half_n, h, True).wait_recv()
        chain_source(s, arrival[1:])
        chain_relay(s, 0)

        @pl.when(pos == 0)
        def _():
            colb[s, core] = grp[s]

        if s == 0:
            loads[1].wait()
        group = grp[s].reshape(rb, ne)
        for h in range(2):
            rows = pl.ds(h * (m // 2), m // 2)
            value = jnp.dot(interp[rows, :], group, preferred_element_type=F32)
            trc[s, c, h] = value.astype(BF16)
            for d in range(2):
                copy = ring(trc, t_ss, t_rs, s, d, 1, h)
                copy.start()
                waits.append((None, copy))

        def trace_step(t):
            for i in range(2):
                for d in range(2):
                    h = halves(d, t)
                    if i < len(h):
                        ring(trc, t_ss, t_rs, s, d, t - 1, h[i], True).wait_recv()
                        copy = ring(trc, t_ss, t_rs, s, d, t, h[i])
                        copy.start()
                        waits.append((None, copy))
            for d in range(2):
                for h in halves(d, t - 1):
                    if h not in halves(d, t):
                        ring(trc, t_ss, t_rs, s, d, t - 1, h, True).wait_recv()

        chain_relay(s, 1)
        for t in range(2, half_n + 1):
            trace_step(t)
        chain_relay(s, 2)
        for delta in range(n):
            chain_done(s, (c + delta) % n, delta)
        chain_sent(s)

        column = colb[s].reshape(2 * rb, ne)
        for i in range(tiles):
            if s == 0:
                loads[2 + i].wait()
            rows = pl.ds(i * tile, tile)
            acc[rows, :] = jnp.dot(surf[rows, :], column, preferred_element_type=F32)

        if s == 0:
            loads[-1].wait()
        own = trc[s, c].reshape(m, ne)
        combined = jnp.dot(dtn[...], own, preferred_element_type=F32)
        combined = combined + (1.0 + face_weight * NADJ) * own.astype(F32)
        for d in range(2):
            for h in halves(d, half_n):
                ring(trc, t_ss, t_rs, s, d, half_n, h, True).wait_recv()
        neighbours = counts[0] * trc[s, 0].reshape(m, ne).astype(F32)
        for p in range(1, n):
            neighbours = neighbours + counts[p] * trc[s, p].reshape(m, ne).astype(F32)
        response = combined - face_weight * neighbours
        turned = response.T.astype(BF16)
        volume = jnp.dot(turned, interp[...], preferred_element_type=F32)
        part[...] = (acc[...] + volume.T).reshape(n, 2, hs, ne)

        def summing(d, t, h):
            k = (s, d, t - 1, h)
            return remote(sbuf.at[k], rbuf.at[k], r_ss.at[k], r_rs.at[k], right if d == 0 else left)

        for t in range(half_n, 0, -1):
            for i in range(2):
                for d in range(2):
                    hh = halves(d, t)[:: -1 if t == half_n - 1 else 1]
                    if i < len(hh):
                        h = hh[i]
                        target = (c + t) % n if d == 0 else (c + n - t) % n
                        value = part[target, h]
                        if t < half_n and h in halves(d, t + 1):
                            summing(d, t + 1, h).wait_recv()
                            value = value + rbuf[s, d, t, h].astype(F32)
                        sbuf[s, d, t - 1, h] = value.astype(BF16)
                        copy = summing(d, t, h)
                        copy.start()
                        waits.append((None, copy))
        for h in range(2):
            rows = pl.ds(h * hs, hs)
            total = part[c, h]
            for d in range(2):
                summing(d, 1, h).wait_recv()
                total = total + rbuf[s, d, 0, h].astype(F32)
            current = base[rows, :]
            residual = exc[rows, :] - current - total
            updated = current + damping * residual
            if s + 1 < ITERS:
                send_own(s + 1, h, updated)
            res_ref[rows, :] = residual
            sol_ref[rows, :] = updated

    for condition, copy in waits:
        if condition is None:
            copy.wait_send()
        else:
            pl.when(condition)(copy.wait_send)


def local(surface, excitation, dtn_blocks, interp_blocks, adjacency):
    R, n = lax.axis_size("row"), lax.axis_size("col")
    shard, ne = excitation.shape
    m, rb = interp_blocks.shape[1:]
    hs = shard // 2
    tile = min(512, surface.shape[0])
    assert R == 2 * n and n % 2 == 0 and n & (n - 1) == 0
    hops = n // 2
    vmem, hbm = pltpu.VMEM, pl.BlockSpec(memory_space=pl.ANY)
    dma = pltpu.SemaphoreType.DMA
    out = jax.ShapeDtypeStruct((shard, ne), F32)
    S = ITERS
    ring_sems = [dma((S, 2, hops, 2))] * 2
    chain_sems = [dma((S, n, 2))] * 2
    return pl.pallas_call(
        functools.partial(kernel, R, n, tile),
        out_shape=(out, out),
        in_specs=[hbm, hbm, hbm, hbm, pl.BlockSpec(memory_space=pltpu.SMEM)],
        out_specs=(pl.BlockSpec(memory_space=vmem),) * 2,
        scratch_shapes=[
            vmem((shard, ne), F32),
            vmem((m, rb), BF16),
            vmem(surface.shape, BF16),
            vmem((m, m), BF16),
            vmem((S, n, 2, hs, ne), BF16),
            vmem((S, 2, n, 2, hs, ne), BF16),
            vmem((S, n, 2, m // 2, ne), BF16),
            vmem((rb, ne), F32),
            vmem((n, 2, hs, ne), F32),
            vmem((S, 2, hops, 2, hs, ne), BF16),
            vmem((S, 2, hops, 2, hs, ne), BF16),
            dma((3 + surface.shape[0] // tile,)),
            *ring_sems, *ring_sems, *chain_sems, *chain_sems, *ring_sems,
        ],
        compiler_params=pltpu.CompilerParams(
            collective_id=0, has_side_effects=True, vmem_limit_bytes=60 * 2**20
        ),
    )(excitation, interp_blocks.reshape(m, rb), surface, dtn_blocks.reshape(m, m), adjacency)


def solution(mesh):
    in_specs = (
        P("row", "col"),
        P(("row", "col"), None),
        P(("row", "col"), None, None),
        P(("row", "col"), None, None),
        P(("row", "col"), None),
    )
    out_specs = (P(("row", "col"), None), P(("row", "col"), None))
    return jax.shard_map(local, mesh=mesh, in_specs=in_specs, out_specs=out_specs, check_vma=False)
```

profile of v0, /device:TPU:0, one launch (start us, length us, event | category | flops | bytes accessed | tf_op | source)
XLA Modules:
  0.0 109.5 jit_solution(14579126612862534791)
XLA Ops:
  0.6 105.5 %shard_map.68 = (f32[512,128]{1,0:T(8,128)}, f32[512,128]{1,0:T(8,128)}) custom-call(f32[512,128]{1,0:T(8,128)} %exc_hbm.1, bf16[1024,2048]{1,0:T(8,128)(2,1)} %bitcast.2, bf16[2048,4096]{1,0:T(8,128)(2,1)} %surf_hbm.1, bf16[1024,1024]{1,0:T(8,128)(2,1)} %bitcast.3, s32[1,6]{1,0:T(1,128)} %adj.1), custom_call_target="tpu_custom_call" | custom-call | tf_op jit(solution)/shard_map/pallas_call | solution.py:308
  106.1 1.7 %copy.9 = f32[512,128]{1,0:T(8,128)} copy(f32[512,128]{1,0:T(8,128)} %get-tuple-element.4) | data formatting | bytes 524288
  107.8 1.7 %copy.10 = f32[512,128]{1,0:T(8,128)} copy(f32[512,128]{1,0:T(8,128)} %get-tuple-element.5) | data formatting | bytes 524288
where the time goes:
time: 110 us; the launch traced here: 109 us
  Pallas kernels  106 us (96%)
  local copies, waits for them, and re-layouts  3.34 us (3%)
    pallas_call x1, Pallas kernels, local(): pl.pallas_call(functools.partial(kernel, R, n, tile), out_shape=(out, out...  106 us
    unnamed x2, local copies, waits for them, and re-layouts  3.34 us

commit v1 on v0

v1 whole, which is shorter than its diff:
```python
import functools

import jax
import jax.numpy as jnp
from jax import lax
from jax.experimental import pallas as pl
from jax.experimental.pallas import tpu as pltpu
from jax.sharding import PartitionSpec as P

ITERS = 2
NADJ = 6
STAGGER = 0

damping = 0.25
face_weight = 0.25
F32, BF16 = jnp.float32, jnp.bfloat16


def xor(a, b, bits):
    total = 0
    for i in range(bits):
        x, y = a // 2**i % 2, b // 2**i % 2
        total = total + (x + y - 2 * x * y) * 2**i
    return total


def gray(p, bits):
    return xor(p, p // 2, bits)


def ungray(g, bits):
    total, above = 0, 0
    for i in reversed(range(bits)):
        bit = g // 2**i % 2
        above = above + bit - 2 * above * bit
        total = total + above * 2**i
    return total


def kernel(
    R, n, pieces, tile,
    exc_hbm, interp_hbm, surf_hbm, dtn_hbm, adj,
    sol_ref, res_ref,
    exc, interp, surf, dtn, grp, colb, trc, acc, part, sbuf, rbuf, nbr, psend, precv, cnt,
    load_sem, g_ss, g_rs, t_ss, t_rs, c_ss, c_rs, h_ss, h_rs, r_ss, r_rs, p_ss, p_rs, n_ss, n_rs,
):
    bits = n.bit_length() - 1
    mid = n // 2
    _, _, hs, ne = grp.shape[1:]
    m, rb = interp.shape
    shard = 2 * hs
    ps = m // pieces
    r, c = lax.axis_index("row"), lax.axis_index("col")
    core, chip = r % 2, r // 2
    pos = ungray(xor(chip, c, bits), bits)
    right, left = (r, (c + 1) % n), (r, (c + n - 1) % n)
    partner = (chip * 2 + 1 - core, c)
    gnext = (xor(gray((pos + 1) % n, bits), c, bits) * 2 + core, c)
    gprev = (xor(gray((pos + n - 1) % n, bits), c, bits) * 2 + core, c)

    loads = [
        pltpu.make_async_copy(exc_hbm, exc, load_sem.at[0]),
        pltpu.make_async_copy(interp_hbm, interp, load_sem.at[1]),
    ]
    tiles = surf.shape[0] // tile
    for i in range(tiles):
        rows = pl.ds(i * tile, tile)
        loads.append(pltpu.make_async_copy(surf_hbm.at[rows], surf.at[rows], load_sem.at[3 + i]))
    loads.append(pltpu.make_async_copy(dtn_hbm, dtn, load_sem.at[2]))
    for load in loads:
        load.start()

    def counts_go(q, j):
        return (mid <= q < j) or (j < q <= mid - 1)

    barrier = pltpu.get_barrier_semaphore()

    def greet(device):
        pl.semaphore_signal(barrier, inc=1, device_id=device, device_id_type=pl.DeviceIdType.MESH)

    for device in (partner, gnext, gprev):
        greet(device)
    expected = 3
    for q in range(n):
        others = [j for j in range(n) if abs(q - j) == 1 or counts_go(q, j) or counts_go(j, q)]

        @pl.when(c == q)
        def _():
            for j in others:
                greet((r, j))

        expected = expected + jnp.where(c == q, len(others), 0)
    pl.semaphore_wait(barrier, expected)

    def remote(src, dst, ss, rs, device):
        return pltpu.make_async_remote_copy(
            src_ref=src, dst_ref=dst, send_sem=ss, recv_sem=rs,
            device_id=device, device_id_type=pl.DeviceIdType.MESH,
        )

    waits = []

    def later(condition, copy):
        waits.append((condition, copy))

    def hop(buf, ss, rs, s, d, t, p, receive=False):
        step = t if receive else t - 1
        owner = (c + n - step) % n if d == 0 else (c + step) % n
        block = buf.at[s, owner, p]
        return remote(block, block, ss.at[s, d, t - 1, p], rs.at[s, d, t - 1, p], right if d == 0 else left)

    def sends(d, t):
        if d == 0:
            return jnp.logical_and(c >= t - 1, c <= n - 2)
        return jnp.logical_and(c <= n - t, c >= 1)

    def receives(d, t):
        return c >= t if d == 0 else c <= n - 1 - t

    def valid(d, t):
        return (c >= 0) if t == 0 else receives(d, t)

    def owner_of(d, t):
        return (c + n - t) % n if d == 0 else (c + t) % n

    def chain_copies(src, s, owner, h):
        block = src.at[owner, h]
        dst = colb.at[s, core, owner, h]
        return (
            remote(block, dst, c_ss.at[s, owner, h], c_rs.at[s, owner, h], gnext if h == 0 else gprev),
            remote(block, dst, h_ss.at[s, owner, h], h_rs.at[s, owner, h], partner),
        )

    def slots(t):
        return [(0, 0)] if t == 0 else [(0, t), (1, t)]

    def chain_source(s, t):
        for d, t in slots(t):
            @pl.when(jnp.logical_and(pos == 0, valid(d, t)))
            def _():
                for h in range(2):
                    on, share = chain_copies(grp.at[s], s, owner_of(d, t), h)
                    on.start()
                    share.start()

    def chain_relay(s, tick):
        for q in range(1, n):
            todo = []
            for t in range(n):
                for h in range(2):
                    if t + (q if h == 0 else n - q) == tick:
                        todo += [(d, t, h) for d, t in slots(t)]
            for d, t, h in todo:
                @pl.when(jnp.logical_and(pos == q, valid(d, t)))
                def _():
                    on, share = chain_copies(colb.at[s, core], s, owner_of(d, t), h)
                    on.wait_recv()
                    if q != (n - 1 if h == 0 else 1):
                        on.start()
                    share.start()

    def chain_sent(s):
        for owner in range(n):
            for h in range(2):
                copies = functools.partial(chain_copies, colb.at[s, core], s, owner, h)
                later(lambda h=h: pos != (n - 1 if h == 0 else 1), lambda copies=copies: copies()[0])
                later(None, lambda copies=copies: copies()[1])

    def shared(s, owner):
        for h in range(2):
            block = colb.at[s, 1 - core, owner, h]
            remote(block, block, h_ss.at[s, owner, h], h_rs.at[s, owner, h], partner).wait_recv()

    ranks = [sorted(range(n), key=lambda o: (abs(o - q), o)) for q in range(n)]
    owner_at = []
    for k in range(n):
        owner = ranks[0][k]
        for q in range(1, n):
            owner = jnp.where(c == q, ranks[q][k], owner)
        owner_at.append(owner)

    for p in range(n):
        count = jnp.float32(0)
        for k in range(NADJ):
            count = count + jnp.where(adj[0, k] % n == p, 1.0, 0.0).astype(F32)
        cnt[c, p] = jnp.full((8, ne), count, F32)

    def count_copy(j, q):
        return remote(cnt.at[j], cnt.at[j], n_ss.at[q], n_rs.at[j], (r, q))

    for j in range(n):
        takers = [q for q in range(n) if counts_go(q, j)]
        if takers:
            @pl.when(c == j)
            def _():
                for q in takers:
                    count_copy(j, q).start()
            for q in takers:
                later(lambda j=j: c == j, lambda j=j, q=q: count_copy(j, q))

    def send_own(s, h, value):
        grp[s, c, h] = value.astype(BF16)
        for d in range(2):
            copy = hop(grp, g_ss, g_rs, s, d, 1, h)
            pl.when(sends(d, 1))(copy.start)
            later(lambda d=d: sends(d, 1), lambda d=d: hop(grp, g_ss, g_rs, s, d, 1, h))

    def gather(s):
        chain_source(s, 0)
        for t in range(1, n):
            for p in range(2):
                for d in range(2):
                    @pl.when(receives(d, t))
                    def _():
                        hop(grp, g_ss, g_rs, s, d, t, p, True).wait_recv()
                    if t < n - 1:
                        copy = hop(grp, g_ss, g_rs, s, d, t + 1, p)
                        pl.when(sends(d, t + 1))(copy.start)
                        later(
                            lambda d=d, t=t: sends(d, t + 1),
                            lambda d=d, t=t, p=p: hop(grp, g_ss, g_rs, s, d, t + 1, p),
                        )
            chain_source(s, t)
            chain_relay(s, t)

    def trace_sends(q, d, t):
        a = q if d == 0 else n - 1 - q
        return a <= mid - 1 and a >= t - 1

    def trace_receives(q, d, t):
        a = q if d == 0 else n - 1 - q
        return a <= mid and a >= t

    def trace_hop(s, q, d, t, p, receive=False):
        step = t if receive else t - 1
        owner = q - step if d == 0 else q + step
        block = trc.at[s, owner, p]
        to = (r, q + 1 if d == 0 else q - 1)
        return remote(block, block, t_ss.at[s, d, t - 1, p], t_rs.at[s, d, t - 1, p], to)

    def sum_copy(s, q, d, j, p):
        to = (r, q + 1 if d == 0 else q - 1)
        return remote(psend.at[s, d, j, p], precv.at[s, d, j, p], p_ss.at[s, d, j, p], p_rs.at[s, d, j, p], to)

    def send_traces(s, p):
        for q in range(n):
            @pl.when(c == q)
            def _():
                for d in range(2):
                    if trace_sends(q, d, 1) and 0 <= q + 1 - 2 * d < n:
                        trace_hop(s, q, d, 1, p).start()

    def weighted(s, j, p, owners):
        total = None
        for o in owners:
            term = cnt[j, o, 0:1] * trc[s, o, p].astype(F32)
            total = term if total is None else total + term
        return total

    def forward_traces(s, t):
        for q in range(n):
            todo = [d for d in range(2) if trace_sends(q, d, t + 1) and trace_receives(q, d, t)]
            if todo:
                @pl.when(c == q)
                def _():
                    for p in range(pieces):
                        for d in todo:
                            trace_hop(s, q, d, t, p, True).wait_recv()
                            trace_hop(s, q, d, t + 1, p).start()

    def trace_sums(s, ends):
        for q in range(n):
            far = [d for d in range(2) if (q if d == 0 else n - 1 - q) > mid]
            if bool(far) != ends:
                continue

            @pl.when(c == q)
            def _():
                if s == 0:
                    for j in range(n):
                        if counts_go(q, j):
                            count_copy(j, q).wait_recv()
                for p in range(pieces):
                    value = weighted(s, q, p, [q])
                    for d in range(2):
                        a = q if d == 0 else n - 1 - q
                        behind = list(range(q)) if d == 0 else list(range(q + 1, n))
                        ahead = list(range(n - 1, q, -1)) if d == 0 else list(range(q))
                        if a <= mid:
                            for t in range(1, a + 1):
                                if not (trace_sends(q, d, t + 1) and trace_receives(q, d, t)):
                                    trace_hop(s, q, d, t, p, True).wait_recv()
                        if a >= mid:
                            for j in ahead:
                                if a == mid:
                                    out = weighted(s, j, p, behind + [q])
                                else:
                                    sum_copy(s, q, d, j, p).wait_recv()
                                    out = precv[s, d, j, p].astype(F32) + weighted(s, j, p, [q])
                                psend[s, d, j, p] = out.astype(BF16)
                                sum_copy(s, q, d, j, p).start()
                                later(lambda q=q: c == q, functools.partial(sum_copy, s, q, d, j, p))
                        if a > mid:
                            sum_copy(s, q, d, q, p).wait_recv()
                            value = value + precv[s, d, q, p].astype(F32)
                        elif behind:
                            value = value + weighted(s, q, p, behind)
                    nbr[pl.ds(p * ps, ps), :] = value

    def traces_sent(s):
        for q in range(n):
            for d in range(2):
                for t in range(1, n):
                    if trace_sends(q, d, t) and 0 <= q + 1 - 2 * d < n:
                        for p in range(pieces):
                            later(lambda q=q: c == q, functools.partial(trace_hop, s, q, d, t, p))

    def apply(s, which, k, first):
        owner = owner_at[k]
        if which == "partner":
            shared(s, owner)
            side = 1 - core
        else:
            side = core
        columns = pl.ds(pl.multiple_of(side * rb + owner * shard, 128), shard)
        block = colb[s, side, owner].reshape(shard, ne)
        value = jnp.dot(surf[:, columns], block, preferred_element_type=F32)
        if first:
            acc[...] = value
        else:
            acc[...] += value

    def sum_hop(s, q, d, j, p):
        to = (r, q + 1 if d == 0 else q - 1)
        return remote(sbuf.at[s, d, j, p], rbuf.at[s, d, j, p], r_ss.at[s, d, j, p], r_rs.at[s, d, j, p], to)

    def reduce(s):
        for q in range(n):
            todo = []
            for d in range(2):
                a = q if d == 0 else n - 1 - q
                for b in range(a + 1, n):
                    j = b if d == 0 else n - 1 - b
                    for p in range(2):
                        todo.append((a * 1.8 + (n - 1 - b) * 2 + p, d, j, p))
            todo.sort()

            @pl.when(c == q)
            def _():
                for _, d, j, p in todo:
                    value = part[j, p]
                    if (q if d == 0 else n - 1 - q) > 0:
                        sum_hop(s, q, d, j, p).wait_recv()
                        value = value + rbuf[s, d, j, p].astype(F32)
                    sbuf[s, d, j, p] = value.astype(BF16)
                    sum_hop(s, q, d, j, p).start()
                    later(lambda q=q: c == q, functools.partial(sum_hop, s, q, d, j, p))

    def reduced(s, h):
        for q in range(n):
            @pl.when(c == q)
            def _():
                total = part[q, h]
                for d in range(2):
                    if (q if d == 0 else n - 1 - q) > 0:
                        sum_hop(s, q, d, q, h).wait_recv()
                        total = total + rbuf[s, d, q, h].astype(F32)
                part[q, h] = total
        return part[c, h]

    loads[0].wait()
    if STAGGER:
        @pl.when(core == 1)
        def _():
            for load in loads[1 : 1 + STAGGER]:
                load.wait()
    for h in range(2):
        send_own(0, h, exc[pl.ds(h * hs, hs), :])
    for s in range(ITERS):
        base = exc if s == 0 else sol_ref
        gather(s)

        @pl.when(pos == 0)
        def _():
            colb[s, core] = grp[s]

        if s == 0:
            if STAGGER:
                @pl.when(core == 0)
                def _():
                    for load in loads[1 : 1 + STAGGER]:
                        load.wait()
            else:
                loads[1].wait()
        group = grp[s].reshape(rb, ne)
        for p in range(pieces):
            value = jnp.dot(interp[pl.ds(p * ps, ps), :], group, preferred_element_type=F32)
            trc[s, c, p] = value.astype(BF16)
            send_traces(s, p)
        traces_sent(s)
        chain_relay(s, n)
        if s == 0:
            for load in loads[1 + max(STAGGER, 1) :]:
                load.wait()
        apply(s, "own", 0, True)
        own = trc[s, c].reshape(m, ne)
        combined = jnp.dot(dtn[...], own, preferred_element_type=F32)
        combined = combined + (1.0 + face_weight * NADJ) * own.astype(F32)
        for t in range(1, mid):
            forward_traces(s, t)
        for tick in range(n + 1, 2 * n - 1):
            chain_relay(s, tick)
            apply(s, "own", tick - n, False)
        chain_sent(s)
        trace_sums(s, False)
        for k in range(1 + max(n - 2, 0), n):
            apply(s, "own", k, False)
        for k in range(n):
            apply(s, "partner", k, False)
        trace_sums(s, True)
        turned = (combined - face_weight * nbr[...]).T.astype(BF16)
        volume = jnp.dot(turned, interp[...], preferred_element_type=F32)
        part[...] = (acc[...] + volume.T).reshape(n, 2, hs, ne)
        reduce(s)
        for h in range(2):
            rows = pl.ds(h * hs, hs)
            total = reduced(s, h)
            current = base[rows, :]
            residual = exc[rows, :] - current - total
            updated = current + damping * residual
            if s + 1 < ITERS:
                send_own(s + 1, h, updated)
            res_ref[rows, :] = residual
            sol_ref[rows, :] = updated

    for condition, copy in waits:
        if condition is None:
            copy().wait_send()
        else:
            @pl.when(condition())
            def _():
                copy().wait_send()


def local(surface, excitation, dtn_blocks, interp_blocks, adjacency):
    R, n = lax.axis_size("row"), lax.axis_size("col")
    shard, ne = excitation.shape
    m, rb = interp_blocks.shape[1:]
    hs = shard // 2
    tile = min(512, surface.shape[0])
    pieces = 4
    assert R == 2 * n and n % 2 == 0 and n & (n - 1) == 0
    vmem, hbm = pltpu.VMEM, pl.BlockSpec(memory_space=pl.ANY)
    dma = pltpu.SemaphoreType.DMA
    out = jax.ShapeDtypeStruct((shard, ne), F32)
    S = ITERS
    return pl.pallas_call(
        functools.partial(kernel, R, n, pieces, tile),
        out_shape=(out, out),
        in_specs=[hbm, hbm, hbm, hbm, pl.BlockSpec(memory_space=pltpu.SMEM)],
        out_specs=(pl.BlockSpec(memory_space=vmem),) * 2,
        scratch_shapes=[
            vmem((shard, ne), F32),
            vmem((m, rb), BF16),
            vmem(surface.shape, BF16),
            vmem((m, m), BF16),
            vmem((S, n, 2, hs, ne), BF16),
            vmem((S, 2, n, 2, hs, ne), BF16),
            vmem((S, n, pieces, m // pieces, ne), BF16),
            vmem((rb, ne), F32),
            vmem((n, 2, hs, ne), F32),
            vmem((S, 2, n, 2, hs, ne), BF16),
            vmem((S, 2, n, 2, hs, ne), BF16),
            vmem((m, ne), F32),
            vmem((S, 2, n, pieces, m // pieces, ne), BF16),
            vmem((S, 2, n, pieces, m // pieces, ne), BF16),
            vmem((n, n, 8, ne), F32),
            dma((3 + surface.shape[0] // tile,)),
            *[dma((S, 2, n, 2))] * 2,
            *[dma((S, 2, n, pieces))] * 2,
            *[dma((S, n, 2))] * 4,
            *[dma((S, 2, n, 2))] * 2,
            *[dma((S, 2, n, pieces))] * 2,
            *[dma((n,))] * 2,
        ],
        compiler_params=pltpu.CompilerParams(
            collective_id=0, has_side_effects=True, vmem_limit_bytes=60 * 2**20
        ),
    )(excitation, interp_blocks.reshape(m, rb), surface, dtn_blocks.reshape(m, m), adjacency)


def solution(mesh):
    in_specs = (
        P("row", "col"),
        P(("row", "col"), None),
        P(("row", "col"), None, None),
        P(("row", "col"), None, None),
        P(("row", "col"), None),
    )
    out_specs = (P(("row", "col"), None), P(("row", "col"), None))
    return jax.shard_map(local, mesh=mesh, in_specs=in_specs, out_specs=out_specs, check_vma=False)
```

time: 110 us -> 92.5 us (0.84)
  Pallas kernels: 106 us -> 88.3 us
    pallas_call x1, Pallas kernels: 106 us -> 88.3 us  [local(): pl.pallas_call(functools.partial(kernel, R, n, pieces, tile), out_shape=(...]
where the time goes in v1:
time: 92.5 us; the launch traced here: 92.3 us
  Pallas kernels  88.3 us (95%)
  local copies, waits for them, and re-layouts  3.34 us (4%)
    pallas_call x1, Pallas kernels, local(): pl.pallas_call(functools.partial(kernel, R, n, pieces, tile), out_shape=(...  88.3 us
    unnamed x2, local copies, waits for them, and re-layouts  3.34 us

profile of v1, /device:TPU:0, one launch (start us, length us, event | category | flops | bytes accessed | tf_op | source)
XLA Modules:
  0.0 92.3 jit_solution(4422080999518909750)
XLA Ops:
  0.6 88.3 %shard_map.68 = (f32[512,128]{1,0:T(8,128)}, f32[512,128]{1,0:T(8,128)}) custom-call(f32[512,128]{1,0:T(8,128)} %exc_hbm.1, bf16[1024,2048]{1,0:T(8,128)(2,1)} %bitcast.2, bf16[2048,4096]{1,0:T(8,128)(2,1)} %surf_hbm.1, bf16[1024,1024]{1,0:T(8,128)(2,1)} %bitcast.3, s32[1,6]{1,0:T(1,128)} %adj.1), custom_call_target="tpu_custom_call" | custom-call | tf_op jit(solution)/shard_map/pallas_call | solution.py:457
  89.0 1.7 %copy.9 = f32[512,128]{1,0:T(8,128)} copy(f32[512,128]{1,0:T(8,128)} %get-tuple-element.4) | data formatting | bytes 524288
  90.7 1.7 %copy.10 = f32[512,128]{1,0:T(8,128)} copy(f32[512,128]{1,0:T(8,128)} %get-tuple-element.5) | data formatting | bytes 524288

commit v2 on v1

v2 whole, which is shorter than its diff:
```python
import functools

import jax
import jax.numpy as jnp
from jax import lax
from jax.experimental import pallas as pl
from jax.experimental.pallas import tpu as pltpu
from jax.sharding import PartitionSpec as P

ITERS = 2
NADJ = 6

damping = 0.25
face_weight = 0.25
F32, BF16 = jnp.float32, jnp.bfloat16


def xor(a, b, bits):
    total = 0
    for i in range(bits):
        x, y = a // 2**i % 2, b // 2**i % 2
        total = total + (x + y - 2 * x * y) * 2**i
    return total


def gray(p, bits):
    return xor(p, p // 2, bits)


def ungray(g, bits):
    total, above = 0, 0
    for i in reversed(range(bits)):
        bit = g // 2**i % 2
        above = above + bit - 2 * above * bit
        total = total + above * 2**i
    return total


def kernel(
    R, n, pieces, tile,
    exc_hbm, interp_hbm, surf_hbm, dtn_hbm, adj,
    cur_ref, tot_ref,
    exc, interp, surf, dtn, grp, colb, trc, acc, part, sbuf, rbuf, ebuf, nbr, psend, precv, cnt,
    load_sem, g_ss, g_rs, t_ss, t_rs, c_ss, c_rs, h_ss, h_rs, r_ss, r_rs, e_rs, p_ss, p_rs, n_ss, n_rs,
):
    bits = n.bit_length() - 1
    mid = n // 2
    _, _, hs, ne = grp.shape[1:]
    m, rb = interp.shape
    shard = 2 * hs
    ps = m // pieces
    r, c = lax.axis_index("row"), lax.axis_index("col")
    core, chip = r % 2, r // 2
    pos = ungray(xor(chip, c, bits), bits)
    partner = (chip * 2 + 1 - core, c)
    gnext = (xor(gray((pos + 1) % n, bits), c, bits) * 2 + core, c)
    gprev = (xor(gray((pos + n - 1) % n, bits), c, bits) * 2 + core, c)

    loads = [
        pltpu.make_async_copy(exc_hbm, exc, load_sem.at[0]),
        pltpu.make_async_copy(interp_hbm, interp, load_sem.at[1]),
    ]
    tiles = surf.shape[0] // tile
    for i in range(tiles):
        rows = pl.ds(i * tile, tile)
        loads.append(pltpu.make_async_copy(surf_hbm.at[rows], surf.at[rows], load_sem.at[3 + i]))
    loads.append(pltpu.make_async_copy(dtn_hbm, dtn, load_sem.at[2]))
    for load in loads:
        load.start()

    def counts_go(q, j):
        return (mid <= q < j) or (j < q <= mid - 1)

    barrier = pltpu.get_barrier_semaphore()
    line = [(r, (c + k) % n) for k in range(1, n)]
    for device in [partner, gnext, gprev] + line:
        pl.semaphore_signal(barrier, inc=1, device_id=device, device_id_type=pl.DeviceIdType.MESH)
    pl.semaphore_wait(barrier, n + 2)

    def remote(src, dst, ss, rs, device):
        return pltpu.make_async_remote_copy(
            src_ref=src, dst_ref=dst, send_sem=ss, recv_sem=rs,
            device_id=device, device_id_type=pl.DeviceIdType.MESH,
        )

    waits = []

    def later(condition, copy):
        waits.append((condition, copy))

    def sender(o, q):
        step = 1 if o < q else -1
        return o if o in (0, n - 1) and (o == 0) == (o < q) or q == o + step else q - step

    def ways(o, q):
        return sorted((k for k in range(n) if k != o and sender(o, k) == q), key=lambda k: -abs(k - o))

    def arrival(o, q):
        if o == q:
            return -1
        a, b = (q, o) if o < q else (n - 1 - q, n - 1 - o)
        return n - a + 1 + 0.3 * a if b == 0 else 2 * (a - b)

    ranks = [sorted(range(n), key=lambda o: arrival(o, q)) for q in range(n)]
    owner_at = []
    for k in range(n):
        owner = ranks[0][k]
        for q in range(1, n):
            owner = jnp.where(c == q, ranks[q][k], owner)
        owner_at.append(owner)

    def block_copy(s, o, q, p):
        block = grp.at[s, o, p]
        return remote(block, block, g_ss.at[s, o, q, p], g_rs.at[s, o, p], (r, q))

    def hops(q, h):
        if (q, h) in ((1, 1), (n - 1, 0)):
            return 1
        return q if h == 0 else n - q

    def passes(q, h, up):
        if q == 0:
            return True
        return up == (h == 0) and (q + 1 <= n - 2 if h == 0 else q - 1 >= 2)

    def chain_copy(src, s, owner, h, up):
        k = 0 if up else 1
        return remote(
            src.at[owner, h], colb.at[s, core, owner, h],
            c_ss.at[s, owner, h, k], c_rs.at[s, owner, h], gnext if up else gprev,
        )

    def share_copy(src, s, owner, h):
        return remote(
            src.at[owner, h], colb.at[s, core, owner, h], h_ss.at[s, owner, h], h_rs.at[s, owner, h], partner
        )

    def chain_source(s, k):
        @pl.when(pos == 0)
        def _():
            for h in range(2):
                for up in (True, False):
                    half = h if up else 1 - h
                    chain_copy(grp.at[s], s, owner_at[k], half, up).start()
            for h in range(2):
                share_copy(grp.at[s], s, owner_at[k], h).start()

    def chain_relay(s, tick):
        for q in range(1, n):
            todo = [(k, h) for k in range(n) for h in range(2) if k + hops(q, h) == tick]
            if not todo:
                continue

            @pl.when(pos == q)
            def _():
                for k, h in todo:
                    src, owner = colb.at[s, core], owner_at[k]
                    chain_copy(src, s, owner, h, True).wait_recv()
                    for up in (True, False):
                        if passes(q, h, up):
                            chain_copy(src, s, owner, h, up).start()
                    share_copy(src, s, owner, h).start()

    def chain_sent(s):
        for owner in range(n):
            for h in range(2):
                later(None, functools.partial(share_copy, colb.at[s, core], s, owner, h))
        for q in range(n):
            for h in range(2):
                for up in (True, False):
                    if passes(q, h, up):
                        for owner in range(n):
                            later(
                                lambda q=q: pos == q,
                                functools.partial(chain_copy, colb.at[s, core], s, owner, h, up),
                            )

    def shared(s, owner):
        for h in range(2):
            block = colb.at[s, 1 - core, owner, h]
            remote(block, block, h_ss.at[s, owner, h], h_rs.at[s, owner, h], partner).wait_recv()

    for p in range(n):
        count = jnp.float32(0)
        for k in range(NADJ):
            count = count + jnp.where(adj[0, k] % n == p, 1.0, 0.0).astype(F32)
        cnt[c, p] = jnp.full((8, ne), count, F32)

    def count_copy(j, q):
        return remote(cnt.at[j], cnt.at[j], n_ss.at[q], n_rs.at[j], (r, q))

    for j in range(n):
        takers = [q for q in range(n) if counts_go(q, j)]
        if takers:
            @pl.when(c == j)
            def _():
                for q in takers:
                    count_copy(j, q).start()
            for q in takers:
                later(lambda j=j: c == j, lambda j=j, q=q: count_copy(j, q))

    def send_own(s, h, value):
        grp[s, c, h] = value.astype(BF16)
        for q in range(n):
            @pl.when(c == q)
            def _():
                for k in ways(q, q):
                    block_copy(s, q, k, h).start()

    def gathered(s):
        for q in range(n):
            for o in range(n):
                for k in ways(o, q):
                    for p in range(2):
                        later(lambda q=q: c == q, functools.partial(block_copy, s, o, k, p))

    def gather(s):
        chain_source(s, 0)
        for rank in range(1, n):
            for q in range(n):
                @pl.when(c == q)
                def _():
                    o = ranks[q][rank]
                    for p in range(2):
                        block_copy(s, o, q, p).wait_recv()
                        for k in ways(o, q):
                            block_copy(s, o, k, p).start()
            chain_source(s, rank)
            chain_relay(s, rank)

    def wanted(o, q):
        return (q if o < q else n - 1 - q) <= mid

    def trace_ways(o, q):
        return [k for k in ways(o, q) if wanted(o, k)]

    def trace_copy(s, o, q, p):
        block = trc.at[s, o, p]
        return remote(block, block, t_ss.at[s, o, q, p], t_rs.at[s, o, p], (r, q))

    def sum_copy(s, q, d, j, p):
        to = (r, q + 1 if d == 0 else q - 1)
        return remote(psend.at[s, d, j, p], precv.at[s, d, j, p], p_ss.at[s, d, j, p], p_rs.at[s, d, j, p], to)

    def send_traces(s, p, far):
        for q in range(n):
            todo = [k for k in trace_ways(q, q) if (abs(k - q) > 1) == far or (far and q not in (0, n - 1))]
            todo = [k for k in todo if far or q in (0, n - 1)]
            if todo:
                @pl.when(c == q)
                def _():
                    for k in todo:
                        trace_copy(s, q, k, p).start()

    def weighted(s, j, p, owners):
        total = None
        for o in owners:
            term = cnt[j, o, 0:1] * trc[s, o, p].astype(F32)
            total = term if total is None else total + term
        return total

    def forward_traces(s):
        for q in range(n):
            todo = [o for o in sorted(range(n), key=lambda o: abs(o - q)) if o != q and trace_ways(o, q)]
            if todo:
                @pl.when(c == q)
                def _():
                    for o in todo:
                        for p in range(pieces):
                            trace_copy(s, o, q, p).wait_recv()
                            for k in trace_ways(o, q):
                                trace_copy(s, o, k, p).start()

    def trace_sums(s, ends):
        for q in range(n):
            far = [d for d in range(2) if (q if d == 0 else n - 1 - q) > mid]
            if bool(far) != ends:
                continue

            @pl.when(c == q)
            def _():
                if s == 0:
                    for j in range(n):
                        if counts_go(q, j):
                            count_copy(j, q).wait_recv()
                for p in range(pieces):
                    value = weighted(s, q, p, [q])
                    for d in range(2):
                        a = q if d == 0 else n - 1 - q
                        behind = list(range(q)) if d == 0 else list(range(q + 1, n))
                        ahead = list(range(n - 1, q, -1)) if d == 0 else list(range(q))
                        if a <= mid:
                            for o in behind:
                                if not trace_ways(o, q):
                                    trace_copy(s, o, q, p).wait_recv()
                        if a >= mid:
                            for j in ahead:
                                if a == mid:
                                    out = weighted(s, j, p, behind + [q])
                                else:
                                    sum_copy(s, q, d, j, p).wait_recv()
                                    out = precv[s, d, j, p].astype(F32) + weighted(s, j, p, [q])
                                psend[s, d, j, p] = out.astype(BF16)
                                sum_copy(s, q, d, j, p).start()
                                later(lambda q=q: c == q, functools.partial(sum_copy, s, q, d, j, p))
                        if a > mid:
                            sum_copy(s, q, d, q, p).wait_recv()
                            value = value + precv[s, d, q, p].astype(F32)
                        elif behind:
                            value = value + weighted(s, q, p, behind)
                    nbr[pl.ds(p * ps, ps), :] = value

    def traces_sent(s):
        for q in range(n):
            for o in range(n):
                for k in trace_ways(o, q):
                    for p in range(pieces):
                        later(lambda q=q: c == q, functools.partial(trace_copy, s, o, k, p))

    def apply(s, which, k, first):
        owner = owner_at[k]
        if which == "partner":
            shared(s, owner)
            side = 1 - core
        else:
            side = core
        columns = pl.ds(pl.multiple_of(side * rb + owner * shard, 128), shard)
        block = colb[s, side, owner].reshape(shard, ne)
        value = jnp.dot(surf[:, columns], block, preferred_element_type=F32)
        if first:
            acc[...] = value
        else:
            acc[...] += value

    def sum_hop(s, q, d, j, p):
        if j in (0, n - 1):
            return remote(sbuf.at[s, d, j, p], ebuf.at[s, q, p], r_ss.at[s, d, j, p], e_rs.at[s, q, p], (r, j))
        to = (r, q + 1 if d == 0 else q - 1)
        return remote(sbuf.at[s, d, j, p], rbuf.at[s, d, j, p], r_ss.at[s, d, j, p], r_rs.at[s, d, j, p], to)

    def reduce(s):
        for q in range(n):
            todo = []
            for d in range(2):
                a = q if d == 0 else n - 1 - q
                for b in range(a + 1, n):
                    j = b if d == 0 else n - 1 - b
                    if b < n - 1:
                        when = n - b + (n if a else 0)
                    else:
                        when = 0 if a else n - 1.5
                    todo += [(when, p, d, j) for p in range(2)]
            todo.sort()

            @pl.when(c == q)
            def _():
                for _, p, d, j in todo:
                    value = part[j, p]
                    if j not in (0, n - 1) and (q if d == 0 else n - 1 - q) > 0:
                        sum_hop(s, q, d, j, p).wait_recv()
                        value = value + rbuf[s, d, j, p].astype(F32)
                    sbuf[s, d, j, p] = value.astype(BF16)
                    sum_hop(s, q, d, j, p).start()
            for _, p, d, j in todo:
                later(lambda q=q: c == q, functools.partial(sum_hop, s, q, d, j, p))

    def reduced(s, h):
        for q in range(n):
            @pl.when(c == q)
            def _():
                total = part[q, h]
                if q in (0, n - 1):
                    for o in sorted(range(n), key=lambda o: abs(o - q))[1:]:
                        sum_hop(s, o, 0 if o < q else 1, q, h).wait_recv()
                        total = total + ebuf[s, o, h].astype(F32)
                else:
                    for d in range(2):
                        sum_hop(s, q, d, q, h).wait_recv()
                        total = total + rbuf[s, d, q, h].astype(F32)
                part[q, h] = total
        return part[c, h]

    loads[0].wait()
    for h in range(2):
        send_own(0, h, exc[pl.ds(h * hs, hs), :])
    for s in range(ITERS):
        gather(s)
        gathered(s)

        @pl.when(pos == 0)
        def _():
            colb[s, core] = grp[s]

        if s == 0:
            loads[1].wait()
        group = grp[s].reshape(rb, ne)
        for p in range(pieces):
            value = jnp.dot(interp[pl.ds(p * ps, ps), :], group, preferred_element_type=F32)
            trc[s, c, p] = value.astype(BF16)
            send_traces(s, p, True)
        for p in range(pieces):
            send_traces(s, p, False)
        traces_sent(s)
        if s == 0:
            for load in loads[2:]:
                load.wait()
        apply(s, "own", 0, True)
        own = trc[s, c].reshape(m, ne)
        combined = jnp.dot(dtn[...], own, preferred_element_type=F32)
        combined = combined + (1.0 + face_weight * NADJ) * own.astype(F32)
        apply(s, "own", 1, False)
        chain_relay(s, n)
        forward_traces(s)
        trace_sums(s, False)
        for tick in range(n + 1, 2 * n - 2):
            chain_relay(s, tick)
        chain_sent(s)
        for k in range(2, n):
            apply(s, "own", k, False)
        for k in range(n):
            apply(s, "partner", k, False)
        trace_sums(s, True)
        turned = (combined - face_weight * nbr[...]).T.astype(BF16)
        volume = jnp.dot(turned, interp[...], preferred_element_type=F32)
        part[...] = (acc[...] + volume.T).reshape(n, 2, hs, ne)
        reduce(s)
        for h in range(2):
            rows = pl.ds(h * hs, hs)
            total = reduced(s, h)
            if s + 1 < ITERS:
                current = exc[rows, :] if s == 0 else cur_ref[rows, :]
                updated = current + damping * (exc[rows, :] - current - total)
                send_own(s + 1, h, updated)
                cur_ref[rows, :] = updated
            else:
                tot_ref[rows, :] = total

    for condition, copy in waits:
        if condition is None:
            copy().wait_send()
        else:
            @pl.when(condition())
            def _():
                copy().wait_send()


def local(surface, excitation, dtn_blocks, interp_blocks, adjacency):
    R, n = lax.axis_size("row"), lax.axis_size("col")
    shard, ne = excitation.shape
    m, rb = interp_blocks.shape[1:]
    hs = shard // 2
    tile = min(512, surface.shape[0])
    pieces = 4
    assert R == 2 * n and n >= 4 and n & (n - 1) == 0
    vmem, hbm = pltpu.VMEM, pl.BlockSpec(memory_space=pl.ANY)
    dma = pltpu.SemaphoreType.DMA
    out = jax.ShapeDtypeStruct((shard, ne), F32)
    S = ITERS
    current, total = pl.pallas_call(
        functools.partial(kernel, R, n, pieces, tile),
        out_shape=(out, out),
        in_specs=[hbm, hbm, hbm, hbm, pl.BlockSpec(memory_space=pltpu.SMEM)],
        out_specs=(pl.BlockSpec(memory_space=vmem),) * 2,
        scratch_shapes=[
            vmem((shard, ne), F32),
            vmem((m, rb), BF16),
            vmem(surface.shape, BF16),
            vmem((m, m), BF16),
            vmem((S, n, 2, hs, ne), BF16),
            vmem((S, 2, n, 2, hs, ne), BF16),
            vmem((S, n, pieces, m // pieces, ne), BF16),
            vmem((rb, ne), F32),
            vmem((n, 2, hs, ne), F32),
            vmem((S, 2, n, 2, hs, ne), BF16),
            vmem((S, 2, n, 2, hs, ne), BF16),
            vmem((S, n, 2, hs, ne), BF16),
            vmem((m, ne), F32),
            vmem((S, 2, n, pieces, m // pieces, ne), BF16),
            vmem((S, 2, n, pieces, m // pieces, ne), BF16),
            vmem((n, n, 8, ne), F32),
            dma((3 + surface.shape[0] // tile,)),
            dma((S, n, n, 2)),
            dma((S, n, 2)),
            dma((S, n, n, pieces)),
            dma((S, n, pieces)),
            dma((S, n, 2, 2)),
            *[dma((S, n, 2))] * 3,
            *[dma((S, 2, n, 2))] * 2,
            dma((S, n, 2)),
            *[dma((S, 2, n, pieces))] * 2,
            *[dma((n,))] * 2,
        ],
        compiler_params=pltpu.CompilerParams(
            collective_id=0, has_side_effects=True, vmem_limit_bytes=60 * 2**20
        ),
    )(excitation, interp_blocks.reshape(m, rb), surface, dtn_blocks.reshape(m, m), adjacency)
    residual = excitation - current - total
    return current + damping * residual, residual


def solution(mesh):
    in_specs = (
        P("row", "col"),
        P(("row", "col"), None),
        P(("row", "col"), None, None),
        P(("row", "col"), None, None),
        P(("row", "col"), None),
    )
    out_specs = (P(("row", "col"), None), P(("row", "col"), None))
    return jax.shard_map(local, mesh=mesh, in_specs=in_specs, out_specs=out_specs, check_vma=False)
```

time: 92.5 us -> 89.6 us (0.969)
  local copies, waits for them, and re-layouts: 3.34 us -> 0.01 us
  other arithmetic: 0 us -> 1.86 us
  Pallas kernels: 88.3 us -> 86.5 us
    unnamed x2, local copies, waits for them, and re-layouts: 3.34 us -> 0.01 us
    add x0 -> x1, other arithmetic: none -> 1.86 us  [local(): return (current + damping * residual, residual)]
    pallas_call x1, Pallas kernels: 88.3 us -> 86.5 us  [local(): pl.pallas_call(functools.partial(kernel, R, n, pieces, tile), out_shape=(...]
where the time goes in v2:
time: 89.6 us; the launch traced here: 89 us
  Pallas kernels  86.5 us (97%)
  other arithmetic  1.86 us (2%)
    pallas_call x1, Pallas kernels, local(): pl.pallas_call(functools.partial(kernel, R, n, pieces, tile), out_shape=(...  86.5 us
    add x1, other arithmetic, local(): return (current + damping * residual, residual)  1.86 us

profile of v2, /device:TPU:0, one launch (start us, length us, event | category | flops | bytes accessed | tf_op | source)
XLA Modules:
  0.0 89.0 jit_solution(10469177477162547319)
XLA Ops:
  0.6 0.0 copy-start
  0.6 86.5 %shard_map.68 = (f32[512,128]{1,0:T(8,128)}, f32[512,128]{1,0:T(8,128)}) custom-call(f32[512,128]{1,0:T(8,128)} %exc_hbm.1, bf16[1024,2048]{1,0:T(8,128)(2,1)} %bitcast.2, bf16[2048,4096]{1,0:T(8,128)(2,1)} %surf_hbm.1, bf16[1024,1024]{1,0:T(8,128)(2,1)} %bitcast.3, s32[1,6]{1,0:T(1,128)} %adj.1), custom_call_target="tpu_custom_call" | custom-call | tf_op jit(solution)/shard_map/pallas_call | solution.py:459
  87.2 0.0 copy-done
  87.2 1.9 %multiply_add_fusion = (f32[512,128]{1,0:T(8,128)}, f32[512,128]{1,0:T(8,128)}) fusion(f32[512,128]{1,0:T(8,128)} %get-tuple-element.4, f32[512,128]{1,0:T(8,128)} %get-tuple-element.5, f32[512,128]{1,0:T(8,128)S(1)} %copy-done), kind=kLoop, calls=%fused_computation | loop fusion | flops 262144 | bytes 1310720 | tf_op jit(solution)/shard_map/add | solution.py:498
Async XLA Ops:
  0.6 86.5 %copy-start = (f32[512,128]{1,0:T(8,128)S(1)}, f32[512,128]{1,0:T(8,128)}, u32[]{:S(2)}) copy-start(f32[512,128]{1,0:T(8,128)} %exc_hbm.1) | copy-start | bytes 786436

commit v3 on v2

--- a/solution.py
+++ b/solution.py
@@ -65,8 +65,7 @@
         rows = pl.ds(i * tile, tile)
         loads.append(pltpu.make_async_copy(surf_hbm.at[rows], surf.at[rows], load_sem.at[3 + i]))
     loads.append(pltpu.make_async_copy(dtn_hbm, dtn, load_sem.at[2]))
-    for load in loads:
-        load.start()
+    loads[0].start()
 
     def counts_go(q, j):
         return (mid <= q < j) or (j < q <= mid - 1)
@@ -83,23 +82,22 @@
             device_id=device, device_id_type=pl.DeviceIdType.MESH,
         )
 
-    waits = []
+    waits = {None: []}
 
     def later(condition, copy):
-        waits.append((condition, copy))
+        waits.setdefault(condition, []).append(copy)
 
     def sender(o, q):
         step = 1 if o < q else -1
         return o if o in (0, n - 1) and (o == 0) == (o < q) or q == o + step else q - step
 
     def ways(o, q):
-        return sorted((k for k in range(n) if k != o and sender(o, k) == q), key=lambda k: -abs(k - o))
+        return [k for k in (q - 1, q + 1) if 0 <= k < n and abs(k - o) > abs(q - o)]
 
     def arrival(o, q):
         if o == q:
             return -1
-        a, b = (q, o) if o < q else (n - 1 - q, n - 1 - o)
-        return n - a + 1 + 0.3 * a if b == 0 else 2 * (a - b)
+        return abs(o - q)
 
     ranks = [sorted(range(n), key=lambda o: arrival(o, q)) for q in range(n)]
     owner_at = []
@@ -171,7 +169,7 @@
                     if passes(q, h, up):
                         for owner in range(n):
                             later(
-                                lambda q=q: pos == q,
+                                ("pos", q),
                                 functools.partial(chain_copy, colb.at[s, core], s, owner, h, up),
                             )
 
@@ -197,7 +195,7 @@
                 for q in takers:
                     count_copy(j, q).start()
             for q in takers:
-                later(lambda j=j: c == j, lambda j=j, q=q: count_copy(j, q))
+                later(("c", j), lambda j=j, q=q: count_copy(j, q))
 
     def send_own(s, h, value):
         grp[s, c, h] = value.astype(BF16)
@@ -212,7 +210,7 @@
             for o in range(n):
                 for k in ways(o, q):
                     for p in range(2):
-                        later(lambda q=q: c == q, functools.partial(block_copy, s, o, k, p))
+                        later(("c", q), functools.partial(block_copy, s, o, k, p))
 
     def gather(s):
         chain_source(s, 0)
@@ -232,7 +230,8 @@
         return (q if o < q else n - 1 - q) <= mid
 
     def trace_ways(o, q):
-        return [k for k in ways(o, q) if wanted(o, k)]
+        near = [k for k in range(n) if k != o and sender(o, k) == q]
+        return [k for k in sorted(near, key=lambda k: -abs(k - o)) if wanted(o, k)]
 
     def trace_copy(s, o, q, p):
         block = trc.at[s, o, p]
@@ -302,7 +301,7 @@
                                     out = precv[s, d, j, p].astype(F32) + weighted(s, j, p, [q])
                                 psend[s, d, j, p] = out.astype(BF16)
                                 sum_copy(s, q, d, j, p).start()
-                                later(lambda q=q: c == q, functools.partial(sum_copy, s, q, d, j, p))
+                                later(("c", q), functools.partial(sum_copy, s, q, d, j, p))
                         if a > mid:
                             sum_copy(s, q, d, q, p).wait_recv()
                             value = value + precv[s, d, q, p].astype(F32)
@@ -315,7 +314,7 @@
             for o in range(n):
                 for k in trace_ways(o, q):
                     for p in range(pieces):
-                        later(lambda q=q: c == q, functools.partial(trace_copy, s, o, k, p))
+                        later(("c", q), functools.partial(trace_copy, s, o, k, p))
 
     def apply(s, which, k, first):
         owner = owner_at[k]
@@ -362,7 +361,7 @@
                     sbuf[s, d, j, p] = value.astype(BF16)
                     sum_hop(s, q, d, j, p).start()
             for _, p, d, j in todo:
-                later(lambda q=q: c == q, functools.partial(sum_hop, s, q, d, j, p))
+                later(("c", q), functools.partial(sum_hop, s, q, d, j, p))
 
     def reduced(s, h):
         for q in range(n):
@@ -381,6 +380,8 @@
         return part[c, h]
 
     loads[0].wait()
+    for load in loads[1:]:
+        load.start()
     for h in range(2):
         send_own(0, h, exc[pl.ds(h * hs, hs), :])
     for s in range(ITERS):
@@ -435,12 +436,12 @@
             else:
                 tot_ref[rows, :] = total
 
-    for condition, copy in waits:
-        if condition is None:
-            copy().wait_send()
-        else:
-            @pl.when(condition())
-            def _():
+    for copy in waits.pop(None):
+        copy().wait_send()
+    for (axis, q), copies in waits.items():
+        @pl.when((c if axis == "c" else pos) == q)
+        def _():
+            for copy in copies:
                 copy().wait_send()
 
 

time: 89.6 us -> 88.2 us (0.984)
  Pallas kernels: 86.5 us -> 85.3 us
    pallas_call x1, Pallas kernels: 86.5 us -> 85.3 us  [local(): pl.pallas_call(functools.partial(kernel, R, n, pieces, tile), out_shape=(...]
where the time goes in v3:
time: 88.2 us; the launch traced here: 87.9 us
  Pallas kernels  85.3 us (97%)
  other arithmetic  1.86 us (2%)
    pallas_call x1, Pallas kernels, local(): pl.pallas_call(functools.partial(kernel, R, n, pieces, tile), out_shape=(...  85.3 us
    add x1, other arithmetic, local(): return (current + damping * residual, residual)  1.86 us

profile of v3, /device:TPU:0, one launch (start us, length us, event | category | flops | bytes accessed | tf_op | source)
XLA Modules:
  0.0 87.9 jit_solution(5786356378029675449)
XLA Ops:
  0.6 0.0 copy-start
  0.6 85.3 %shard_map.68 = (f32[512,128]{1,0:T(8,128)}, f32[512,128]{1,0:T(8,128)}) custom-call(f32[512,128]{1,0:T(8,128)} %exc_hbm.1, bf16[1024,2048]{1,0:T(8,128)(2,1)} %bitcast.2, bf16[2048,4096]{1,0:T(8,128)(2,1)} %surf_hbm.1, bf16[1024,1024]{1,0:T(8,128)(2,1)} %bitcast.3, s32[1,6]{1,0:T(1,128)} %adj.1), custom_call_target="tpu_custom_call" | custom-call | tf_op jit(solution)/shard_map/pallas_call | solution.py:460
  86.0 0.0 copy-done
  86.0 1.9 %multiply_add_fusion = (f32[512,128]{1,0:T(8,128)}, f32[512,128]{1,0:T(8,128)}) fusion(f32[512,128]{1,0:T(8,128)} %get-tuple-element.4, f32[512,128]{1,0:T(8,128)} %get-tuple-element.5, f32[512,128]{1,0:T(8,128)S(1)} %copy-done), kind=kLoop, calls=%fused_computation | loop fusion | flops 262144 | bytes 1310720 | tf_op jit(solution)/shard_map/add | solution.py:499
Async XLA Ops:
  0.6 85.4 %copy-start = (f32[512,128]{1,0:T(8,128)S(1)}, f32[512,128]{1,0:T(8,128)}, u32[]{:S(2)}) copy-start(f32[512,128]{1,0:T(8,128)} %exc_hbm.1) | copy-start | bytes 786436
